TPU v7x, 32 devices: a whole 2x2x4 slice. The times are simulated.
32 devices in a mesh: owner: 4 (over y, x), rows: 8 (over z, core).
Axes of the slice: x: 2, y: 2, z: 4, core: 2. Of those that a mesh axis runs over, the one named last changes fastest.
Arguments:
- train_gate: float32 [64, 2048, 1024], P('owner', 'rows'), may hold values from -0.1875 to 0.1875
- train_up: float32 [64, 2048, 1024], P('owner', 'rows'), may hold values from -0.1875 to 0.1875
- train_down: float32 [64, 1024, 2048], P('owner', None, 'rows'), may hold values from -0.25 to 0.25
- router_weight: float32 [2048, 64], P('rows', 'owner'), may hold values from -0.125 to 0.125
- router_gain: float32 [2048], P('rows'), may hold values from 0.25 to 1.75
Outputs:
- ready_gate: bfloat16 [64, 2048, 1024], P('owner', None, 'rows')
- ready_up: bfloat16 [64, 2048, 1024], P('owner', None, 'rows')
- ready_down: bfloat16 [64, 1024, 2048], P('owner', 'rows')
- scale_gate: float32 [64, 1024], P('owner', 'rows')
- scale_up: float32 [64, 1024], P('owner', 'rows')
- scale_down: float32 [64, 1024], P('owner', 'rows')
- serve_router: bfloat16 [2048, 64], replicated
All inputs are finite; a program needn't handle non-finite values. Where the computation divides by a largest or mean magnitude, that divisor is 1e-20 or more.
Results may differ from a plain program's by a relative error of at most 0.0013.
Values may be sent and summed in bfloat16 or wider, within the bound.
A program may use at most 192 MiB of HBM per device.

v0:
```python
import functools

import jax
import jax.numpy as jnp
from jax import lax
from jax.experimental import pallas as pl
from jax.experimental.pallas import tpu as pltpu
from jax.sharding import PartitionSpec as P

CORES = 2
SLOTS = 4
GROUPS = 4
MESH = pl.DeviceIdType.MESH


def exchange(
    n,
    owners,
    gate,
    up,
    down,
    router,
    out_gate,
    out_up,
    out_down,
    out_scale,
    out_router,
    wide,
    tall,
    send_wide,
    send_tall,
    part,
    arrived,
    inverse,
    load_sem,
    own_sem,
    sum_send,
    sum_recv,
    inv_send,
    inv_recv,
    row_send,
    row_recv,
    col_send,
    col_recv,
    send_sem,
    recv_sem,
):
    me = lax.axis_index("rows")
    home = lax.axis_index("owner")
    experts, rows, _ = gate.shape
    share = out_gate.shape[2]
    slots = min(SLOTS, experts)
    per = max(1, experts // GROUPS)
    groups = experts // per
    chips = n // CORES
    chip = me // CORES
    core = lax.rem(me, CORES)

    def peer(k):
        return lax.rem(me + k, n)

    def remote(src, dst, out_sem, in_sem, **where):
        return pltpu.make_async_remote_copy(
            src_ref=src,
            dst_ref=dst,
            send_sem=out_sem,
            recv_sem=in_sem,
            device_id=where,
            device_id_type=MESH,
        )

    barrier = pltpu.get_barrier_semaphore()
    for k in range(1, n):
        pl.semaphore_signal(barrier, inc=1, device_id={"rows": peer(k)}, device_id_type=MESH)
    for k in range(1, owners):
        pl.semaphore_signal(
            barrier, inc=1, device_id={"owner": lax.rem(home + k, owners)}, device_id_type=MESH
        )

    def load(src, buf, e):
        slot = lax.rem(e, slots)
        kind = 0 if buf is wide else 1
        return pltpu.make_async_copy(src.at[e], buf.at[slot], load_sem.at[kind, slot])

    def fill(src, buf):
        for e in range(slots):
            load(src, buf, e).start()

    def take(src, buf, e, body):
        load(src, buf, e).wait()
        body(e, lax.rem(e, slots))

        @pl.when(e + slots < experts)
        def _():
            load(src, buf, e + slots).start()

    def sums_wide(t):
        def body(e, slot):
            for j in range(n):
                block = wide[slot, :, j * share : (j + 1) * share]
                part[j, t, e] = jnp.sum(jnp.abs(block), axis=0, keepdims=True)

        return body

    def sums_tall(e, slot):
        for j in range(n):
            block = tall[slot, j * share : (j + 1) * share, :]
            part[j, 2, e] = jnp.sum(jnp.abs(block).T, axis=0, keepdims=True)

    def run(src, buf, body):
        fill(src, buf)

        @pl.loop(0, experts)
        def _(e):
            take(src, buf, e, body)

    run(gate, wide, sums_wide(0))

    pl.semaphore_wait(barrier, n - 1 + owners - 1)

    stages = (pl.ds(0, 1), pl.ds(1, 2))

    def sum_copy(stage, to, src):
        return remote(
            part.at[to, stages[stage]],
            arrived.at[src, stages[stage]],
            sum_send.at[stage, to],
            sum_recv.at[stage, src],
            rows=to,
        )

    def inv_copy(stage, to, src):
        block = inverse.at[src, stages[stage]]
        return remote(block, block, inv_send.at[stage, to], inv_recv.at[stage, src], rows=to)

    def send_sums(stage):
        for k in range(1, n):
            sum_copy(stage, peer(k), me).start()

    def send_inverse(stage):
        total = part[me, stages[stage]]
        for k in range(1, n):
            sum_copy(stage, peer(k), peer(k)).wait_recv()
            total = total + arrived[peer(k), stages[stage]]
        scale = total / (rows * n)
        out_scale[stages[stage]] = scale
        inverse[me, stages[stage]] = 1.0 / scale
        for k in range(1, n):
            inv_copy(stage, peer(k), me).start()

    def await_inverse(stage):
        for k in range(1, n):
            inv_copy(stage, peer(k), peer(k)).wait_recv()

    def row_copy(to, src):
        return remote(
            router,
            out_router.at[home, :, pl.ds(pl.multiple_of(src * rows, rows), rows)],
            row_send.at[to],
            row_recv.at[src],
            rows=to,
        )

    def col_copy(to, src):
        return remote(
            out_router.at[src], out_router.at[src], col_send.at[to], col_recv.at[src], owner=to
        )

    send_sums(0)
    fill(gate, wide)
    for k in range(1, n):
        row_copy(peer(k), me).start()
    mine = out_router.at[home, :, pl.ds(pl.multiple_of(me * rows, rows), rows)]
    own_router = pltpu.make_async_copy(router, mine, own_sem.at[0])
    own_router.start()
    send_inverse(0)
    await_inverse(0)

    def block_copy(t, g, to, src):
        some = pl.ds(g * per, per)
        span = pl.ds(pl.multiple_of(src * rows, rows), rows)
        if t < 2:
            piece = send_wide.at[t, to, some]
            dst = (out_gate, out_up)[t].at[some, span, :]
        else:
            piece = send_tall.at[to, some]
            dst = out_down.at[some, :, span]
        return remote(piece, dst, send_sem.at[t, g, to], recv_sem.at[t, g, src], rows=to)

    def own_copy(t):
        span = pl.ds(pl.multiple_of(me * rows, rows), rows)
        if t < 2:
            return pltpu.make_async_copy(
                send_wide.at[t, me], (out_gate, out_up)[t].at[:, span, :], own_sem.at[1 + t]
            )
        return pltpu.make_async_copy(send_tall.at[me], out_down.at[:, :, span], own_sem.at[1 + t])

    def send_at(t, g, d):
        for side in (1, -1):
            there = chip + side * d

            @pl.when((there >= 0) & (there < chips))
            def _():
                for c in range(CORES):
                    block_copy(t, g, there * CORES + lax.rem(core + c, CORES), me).start()

    def ready_wide(t):
        def body(e, slot):
            for j in range(n):
                block = wide[slot, :, j * share : (j + 1) * share]
                send_wide[t, j, e] = (block * inverse[j, t, e]).astype(jnp.bfloat16)

        return body

    def ready_tall(e, slot):
        for j in range(n):
            block = tall[slot, j * share : (j + 1) * share, :]
            factor = jnp.broadcast_to(inverse[j, 2, e], (rows, share)).T
            send_tall[j, e] = (block * factor).astype(jnp.bfloat16)

    def send_near(t, g):
        send_at(t, g, 1)
        for c in range(1, CORES):
            block_copy(t, g, chip * CORES + lax.rem(core + c, CORES), me).start()

    def ready(t, src, buf, body, sent):
        @pl.loop(0, groups)
        def _(g):
            @pl.loop(0, per)
            def _(i):
                take(src, buf, g * per + i, body)

            @pl.when(g < sent)
            def _():
                send_near(t, g)

        own_copy(t).start()

    early = max(1, groups - 1)
    ahead = min(2, groups)
    ready(0, gate, wide, ready_wide(0), early)
    run(up, wide, sums_wide(1))
    run(down, tall, sums_tall)
    send_sums(1)
    fill(up, wide)
    fill(down, tall)
    for g in range(early, groups):
        send_near(0, g)
    send_inverse(1)
    if chips > 2:
        for g in range(ahead):
            send_at(0, g, 2)
    await_inverse(1)
    ready(1, up, wide, ready_wide(1), groups)
    ready(2, down, tall, ready_tall, groups)

    for k in range(1, n):
        row_copy(peer(k), peer(k)).wait_recv()
    own_router.wait()
    for k in range(1, owners):
        col_copy(lax.rem(home + k, owners), home).start()

    if chips > 2:

        @pl.loop(ahead, groups)
        def _(g):
            send_at(0, g, 2)

        for t in (1, 2):

            @pl.loop(0, groups)
            def _(g):
                send_at(t, g, 2)

    @pl.loop(3, max(3, chips))
    def _(d):
        for t in range(3):

            @pl.loop(0, groups)
            def _(g):
                send_at(t, g, d)

    for k in range(1, owners):
        other = lax.rem(home + k, owners)
        col_copy(other, other).wait_recv()
        col_copy(other, home).wait_send()
    for k in range(1, n):
        for stage in range(2):
            sum_copy(stage, peer(k), me).wait_send()
            inv_copy(stage, peer(k), me).wait_send()
        row_copy(peer(k), me).wait_send()
    for t in range(3):
        own_copy(t).wait()

        @pl.loop(0, groups)
        def _(g):
            @pl.loop(1, n)
            def _(k):
                block_copy(t, g, peer(k), peer(k)).wait_recv()
                block_copy(t, g, peer(k), me).wait_send()


def local(n, owners, gate, up, down, router_weight, router_gain):
    experts, rows, width = gate.shape
    share = width // n
    per = max(1, experts // GROUPS)
    groups = experts // per
    slots = min(SLOTS, experts)
    router = (router_weight * router_gain[:, None]).T.astype(jnp.bfloat16)
    anywhere = pl.BlockSpec(memory_space=pl.ANY)
    f32, bf16 = jnp.float32, jnp.bfloat16
    dma = pltpu.SemaphoreType.DMA
    ready_gate, ready_up, ready_down, scales, columns = pl.pallas_call(
        functools.partial(exchange, n, owners),
        name="exchange",
        out_shape=(
            jax.ShapeDtypeStruct((experts, rows * n, share), bf16),
            jax.ShapeDtypeStruct((experts, rows * n, share), bf16),
            jax.ShapeDtypeStruct((experts, share, rows * n), bf16),
            jax.ShapeDtypeStruct((3, experts, 1, share), f32),
            jax.ShapeDtypeStruct((owners, router.shape[0], rows * n), bf16),
        ),
        in_specs=[anywhere] * 4,
        out_specs=(
            anywhere,
            anywhere,
            anywhere,
            pl.BlockSpec(memory_space=pltpu.VMEM),
            anywhere,
        ),
        scratch_shapes=[
            pltpu.VMEM((slots, rows, width), f32),
            pltpu.VMEM((slots, width, rows), f32),
            pltpu.VMEM((2, n, experts, rows, share), bf16),
            pltpu.VMEM((n, experts, share, rows), bf16),
            pltpu.VMEM((n, 3, experts, 1, share), f32),
            pltpu.VMEM((n, 3, experts, 1, share), f32),
            pltpu.VMEM((n, 3, experts, 1, share), f32),
            dma((2, slots)),
            dma((4,)),
            dma((2, n)),
            dma((2, n)),
            dma((2, n)),
            dma((2, n)),
            dma((n,)),
            dma((n,)),
            dma((owners,)),
            dma((owners,)),
            dma((3, groups, n)),
            dma((3, groups, n)),
        ],
        compiler_params=pltpu.CompilerParams(
            collective_id=0, has_side_effects=True, vmem_limit_bytes=58 * 1024 * 1024
        ),
    )(gate, up, down, router)
    serve_router = jnp.transpose(columns, (2, 0, 1)).reshape(rows * n, -1)
    scale_gate, scale_up, scale_down = (scales[t].reshape(experts, share) for t in range(3))
    return (ready_gate, ready_up, ready_down, scale_gate, scale_up, scale_down, serve_router)


def solution(mesh):
    return jax.shard_map(
        functools.partial(local, mesh.shape["rows"], mesh.shape["owner"]),
        mesh=mesh,
        in_specs=(
            P("owner", "rows", None),
            P("owner", "rows", None),
            P("owner", None, "rows"),
            P("rows", "owner"),
            P("rows"),
        ),
        out_specs=(
            P("owner", None, "rows"),
            P("owner", None, "rows"),
            P("owner", "rows", None),
            P("owner", "rows"),
            P("owner", "rows"),
            P("owner", "rows"),
            P(),
        ),
        check_vma=False,
    )
```

profile of v0, /device:TPU:9, one launch (start us, length us, event | category | flops | bytes accessed | tf_op | source)
XLA Modules:
  0.0 590.9 jit_solution(14256768373469901661)
XLA Ops:
  0.6 1.3 fusion.router
  2.0 563.2 %exchange.1 = (bf16[16,2048,128]{2,1,0:T(8,128)(2,1)}, bf16[16,2048,128]{2,1,0:T(8,128)(2,1)}, bf16[16,128,2048]{2,1,0:T(8,128)(2,1)}, f32[3,16,1,128]{3,2,1,0:T(1,128)}, bf16[4,16,2048]{2,1,0:T(8,128)(2,1)}) custom-call(f32[16,256,1024]{2,1,0:T(8,128)} %gate.1, f32[16,256,1024]{2,1,0:T(8,128)} %up.1, f32[16,1024,256]{2,1,0:T(8,128)} %down.1, ...), custom_call_target="tpu_custom_call" | custom-call | tf_op jit(solution)/shard_map/exchange/pallas_call | solution.py:313
  565.2 1.3 fusion.1
  566.5 7.6 %copy.16 = bf16[16,2048,128]{2,1,0:T(8,128)(2,1)} copy(bf16[16,2048,128]{2,1,0:T(8,128)(2,1)} %get-tuple-element.27) | data formatting | bytes 16777216
  574.1 7.6 %copy.17 = bf16[16,2048,128]{2,1,0:T(8,128)(2,1)} copy(bf16[16,2048,128]{2,1,0:T(8,128)(2,1)} %get-tuple-element.28) | data formatting | bytes 16777216
  581.7 0.0 copy-start
  581.7 8.5 %copy.18 = bf16[16,128,2048]{2,1,0:T(8,128)(2,1)} copy(bf16[16,128,2048]{2,1,0:T(8,128)(2,1)} %get-tuple-element.29) | data formatting | bytes 16777216
  590.1 0.0 copy-done
  590.2 0.7 copy.19
Async XLA Ops:
  581.7 8.5 %copy-start = (bf16[4,16,2048]{2,1,0:T(8,128)(2,1)S(1)}, bf16[4,16,2048]{2,1,0:T(8,128)(2,1)}, u32[]{:S(2)}) copy-start(bf16[4,16,2048]{2,1,0:T(8,128)(2,1)} %get-tuple-element.16) | copy-start | bytes 786436
where the time goes:
time: 595 us; the launch traced here: 591 us
  Pallas kernels  563 us (95%)
  local copies, waits for them, and re-layouts  25.7 us (4%)
    pallas_call x1, Pallas kernels, local(): pl.pallas_call(functools.partial(exchange, n, owners), name='exchange', o...  563 us
    unnamed x6, local copies, waits for them, and re-layouts  24.4 us

commit v1 on v0

v1 whole, which is shorter than its diff:
```python
import functools

import jax
import jax.numpy as jnp
from jax import lax
from jax.experimental import pallas as pl
from jax.experimental.pallas import tpu as pltpu
from jax.sharding import PartitionSpec as P

CORES = 2
SLOTS = 4
EARLY = 2
GROUPS = 4
MESH = pl.DeviceIdType.MESH


def groups_of(experts, start):
    per = max(1, experts // GROUPS)
    out = [(e, 1) for e in range(start)]
    at = start
    while at < experts:
        end = min(experts, (at // per + 1) * per)
        out.append((at, end - at))
        at = end
    return out


def plan(experts):
    early = min(EARLY, experts // 2)
    groups = [groups_of(experts, early), groups_of(experts, 0), groups_of(experts, 0)]
    base = [0, len(groups[0]), len(groups[0]) + len(groups[1])]
    return early, groups, base, sum(len(g) for g in groups)


def exchange(
    n,
    owners,
    gate,
    up,
    down,
    router_weight,
    router_gain,
    out_gate,
    out_up,
    out_down,
    scale_gate,
    scale_up,
    scale_down,
    out_router,
    first,
    wide,
    tall,
    send_wide,
    send_tall,
    early_part,
    early_got,
    early_inv,
    part,
    got_side,
    half_sum,
    got_half,
    total,
    inverse,
    weight,
    gain,
    router,
    load_sem,
    early_send,
    early_recv,
    side_send,
    side_recv,
    half_send,
    half_recv,
    total_send,
    total_recv,
    router_send,
    router_recv,
    fwd_send,
    fwd_recv,
    col_send,
    col_recv,
    bulk_send,
    bulk_recv,
):
    me = lax.axis_index("rows")
    home = lax.axis_index("owner")
    experts, rows, width = gate.shape
    share = width // n
    pair = 2 * share
    half = n // 2
    slots = wide.shape[0]
    chips = n // CORES
    half_chips = chips // 2
    chip = me // CORES
    core = lax.rem(me, CORES)
    side = me // half
    member = lax.rem(me, half)
    facing = lax.rem(me + half, n)
    early, groups, base, _ = plan(experts)
    count = rows * n
    srcs = (gate, up, down)
    span = pl.ds(pl.multiple_of(me * rows, rows), rows)

    def peer(k):
        return lax.rem(me + k, n)

    def mate(k):
        return lax.rem(member + k, half)

    def remote(src, dst, out_sem, in_sem, **where):
        return pltpu.make_async_remote_copy(
            src_ref=src,
            dst_ref=dst,
            send_sem=out_sem,
            recv_sem=in_sem,
            device_id=where,
            device_id_type=MESH,
        )

    def load(t, e):
        buf = wide if t < 2 else tall
        slot = lax.rem(e, slots)
        return pltpu.make_async_copy(
            srcs[t].at[e], buf.at[slot], load_sem.at[0 if t < 2 else 1, slot]
        )

    def load_first(e):
        return pltpu.make_async_copy(gate.at[e], first.at[e], load_sem.at[2, e])

    for e in range(early):
        load_first(e).start()

    def fill(t, start):
        for e in range(start, min(start + slots, experts)):
            load(t, e).start()

    def take(t, e, body):
        load(t, e).wait()
        body(e, lax.rem(e, slots))

        @pl.when(e + slots < experts)
        def _():
            load(t, e + slots).start()

    def run(t, start, stop, body):
        @pl.loop(start, stop)
        def _(e):
            take(t, e, body)

    fill(0, early)
    weight_load = pltpu.make_async_copy(router_weight, weight, load_sem.at[3, 0])
    gain_load = pltpu.make_async_copy(router_gain, gain, load_sem.at[3, 1])
    weight_load.start()
    gain_load.start()

    barrier = pltpu.get_barrier_semaphore()
    for k in range(1, n):
        pl.semaphore_signal(barrier, inc=1, device_id={"rows": peer(k)}, device_id_type=MESH)
    for k in range(1, owners):
        pl.semaphore_signal(
            barrier, inc=1, device_id={"owner": lax.rem(home + k, owners)}, device_id_type=MESH
        )

    def put_part(t, e, sums):
        for q in range(half):
            part[q, t, pl.ds(e, 1), :] = sums[:, q * pair : (q + 1) * pair]

    def sums_wide(t):
        def body(e, slot):
            put_part(t, e, jnp.sum(jnp.abs(wide[slot]), axis=0, keepdims=True))

        return body

    def sums_tall(e, slot):
        for q in range(half):
            block = jnp.abs(tall[slot, q * pair : (q + 1) * pair, :])
            folded = block[:, :128]
            for c in range(128, rows, 128):
                folded = folded + block[:, c : c + 128]
            part[q, 2, pl.ds(e, 1), :] = jnp.sum(folded.T, axis=0, keepdims=True)

    for e in range(early):
        load_first(e).wait()
        sums = jnp.sum(jnp.abs(first[e]), axis=0, keepdims=True)
        put_part(0, e, sums)
        for s in range(2):
            early_part[s, pl.ds(e, 1), :] = sums[:, s * (width // 2) : (s + 1) * (width // 2)]

    pl.semaphore_wait(barrier, n - 1 + owners - 1)

    def early_copy(to, src):
        return remote(
            early_part.at[1 - to // half],
            early_got.at[src],
            early_send.at[to],
            early_recv.at[src],
            rows=to,
        )

    for k in range(1, n):
        early_copy(peer(k), me).start()

    run(0, early, experts, sums_wide(0))

    stages = (pl.ds(0, 1), pl.ds(1, 2))

    def side_copy(s, to, src):
        return remote(
            part.at[to, stages[s]],
            got_side.at[src, stages[s]],
            side_send.at[s, to],
            side_recv.at[s, src],
            rows=side * half + to,
        )

    def half_copy(s):
        return remote(
            half_sum.at[stages[s]],
            got_half.at[stages[s]],
            half_send.at[s],
            half_recv.at[s],
            rows=facing,
        )

    def total_copy(s, to, src):
        block = total.at[src, stages[s]]
        return remote(
            block, block, total_send.at[s, to], total_recv.at[s, src], rows=side * half + to
        )

    def sums_side(s):
        for k in range(1, half):
            side_copy(s, mate(k), member).start()

    def sums_across(s):
        acc = part[member, stages[s]]
        for k in range(1, half):
            side_copy(s, mate(k), mate(k)).wait_recv()
            acc = acc + got_side[mate(k), stages[s]]
        half_sum[stages[s]] = acc
        half_copy(s).start()

    def sums_back(s):
        half_copy(s).wait_recv()
        total[member, stages[s]] = half_sum[stages[s]] + got_half[stages[s]]
        for k in range(1, half):
            total_copy(s, mate(k), member).start()

    scales = (scale_gate, scale_up, scale_down)

    def sums_done(s):
        for k in range(1, half):
            total_copy(s, mate(k), mate(k)).wait_recv()
        for t in ((0,), (1, 2))[s]:
            for q in range(half):
                inverse[q, t] = 1.0 / (total[q, t] / count)
            mine = total[me // 2, t] / count
            scales[t][...] = jnp.where(lax.rem(me, 2) == 0, mine[:, :share], mine[:, share:])

    sums_side(0)

    def block_copy(t, g, to, src):
        start, size = groups[t][g]
        some = pl.ds(start, size)
        at = pl.ds(pl.multiple_of(src * rows, rows), rows)
        if t < 2:
            piece = send_wide.at[t, to, some]
            dst = (out_gate, out_up)[t].at[some, at, :]
        else:
            piece = send_tall.at[to, some]
            dst = out_down.at[some, :, at]
        b = base[t] + g
        return remote(piece, dst, bulk_send.at[b, to], bulk_recv.at[b, src], rows=to)

    def send_chip(t, g, there):
        for c in range(CORES):
            block_copy(t, g, there * CORES + lax.rem(core + c, CORES), me).start()

    def send_at(t, g, d):
        first_ones = t == 0 and g < early
        for way in (1, -1):
            there = chip + way * d
            ok = (there >= 0) & (there < chips)
            if first_ones:
                ok = ok & (there // half_chips == chip // half_chips)

            @pl.when(ok)
            def _():
                send_chip(t, g, there)

    def send_near(t, g):
        send_at(t, g, 1)
        for c in range(1, CORES):
            block_copy(t, g, chip * CORES + lax.rem(core + c, CORES), me).start()

    def send_across(g, k):
        there = jnp.where(side == 0, half_chips + k, half_chips - 1 - k)
        send_chip(0, g, there)

    def scaled_pair(t, e, q, block, factor):
        value = (block * factor).astype(jnp.bfloat16)
        for i in range(2):
            send_wide[t, 2 * q + i, e] = value[:, i * share : (i + 1) * share]

    def half_first(e, which, factor_of):
        for p in range(half // 2):
            q = which * (half // 2) + p
            at = pl.ds(pl.multiple_of(q * pair, pair), pair)
            scaled_pair(0, e, q, first[e, :, at], factor_of(p, q))

    def early_factor(e):
        return lambda p, q: early_inv[pl.ds(e, 1), p * pair : (p + 1) * pair]

    def ready_wide(t):
        def body(e, slot):
            for q in range(half):
                scaled_pair(
                    t,
                    e,
                    q,
                    wide[slot, :, q * pair : (q + 1) * pair],
                    inverse[q, t, pl.ds(e, 1), :],
                )

        return body

    def ready_tall(e, slot):
        for q in range(half):
            row = inverse[q, 2, pl.ds(e, 1), :]
            factor = jnp.broadcast_to(row, (128, pair)).T
            for c in range(0, rows, 128):
                block = tall[slot, q * pair : (q + 1) * pair, c : c + 128]
                value = (block * factor).astype(jnp.bfloat16)
                for i in range(2):
                    send_tall[2 * q + i, e, :, c : c + 128] = value[
                        i * share : (i + 1) * share
                    ]

    def own(t, start, stop):
        @pl.loop(start, stop)
        def _(e):
            if t < 2:
                (out_gate, out_up)[t][e, span, :] = send_wide[t, me, e]
            else:
                out_down[e, :, span] = send_tall[me, e]

    def ready(t, g, body):
        start, size = groups[t][g]
        run(t, start, start + size, body)

    acc = early_part[1 - side]
    for k in range(1, n):
        early_copy(peer(k), peer(k)).wait_recv()
        acc = acc + early_got[peer(k)]
    early_inv[...] = 1.0 / (acc / count)

    fill(1, 0)
    half_first(0, 1 - side, early_factor(0))
    send_across(0, 0)
    sums_across(0)
    for k in range(1, half_chips):
        send_across(0, k)
    for e in range(1, early):
        half_first(e, 1 - side, early_factor(e))
    run(1, 0, experts, sums_wide(1))
    fill(0, early)
    sums_back(0)
    for e in range(1, early):
        for k in range(half_chips):
            send_across(e, k)

    weight_load.wait()
    gain_load.wait()
    router[...] = (weight[...] * gain[...]).astype(jnp.bfloat16)
    out_router[home, :, span] = router[...]

    def strip(src):
        return out_router.at[home, :, pl.ds(pl.multiple_of(src * rows, rows), rows)]

    def router_copy(to, src):
        return remote(router, strip(src), router_send.at[to], router_recv.at[src], rows=to)

    def forward_copy(to, src):
        return remote(
            strip(lax.rem(src + half, n)),
            strip(lax.rem(src + half, n)),
            fwd_send.at[to],
            fwd_recv.at[src],
            rows=to,
        )

    def col_copy(to, src):
        return remote(
            out_router.at[src], out_router.at[src], col_send.at[to], col_recv.at[src], owner=to
        )

    for k in range(1, half):
        router_copy(side * half + mate(k), me).start()
    router_copy(facing, me).start()

    sums_done(0)

    for e in range(early):
        half_first(e, side, lambda p, q: inverse[q, 0, pl.ds(e, 1), :])
    for g in range(early):
        send_near(0, g)
    rest = range(early, len(groups[0]))
    for g in rest:
        ready(0, g, ready_wide(0))
        send_near(0, g)
    fill(2, 0)
    own(0, 0, experts)
    run(2, 0, experts, sums_tall)
    fill(1, 0)
    fill(2, 0)

    def spread(t, g, d):
        send_at(t, g, d)

    def two(g):
        if chips > 2:
            send_at(0, g, 2)

    cuts = [list(rest)[:1], list(rest)[1:2], list(rest)[2:]]
    sums_side(1)
    for g in range(early):
        two(g)
    for g in cuts[0]:
        two(g)
    sums_across(1)
    for g in cuts[1]:
        two(g)
    sums_back(1)
    for g in cuts[2]:
        two(g)

    router_copy(facing, facing).wait_recv()
    for k in range(1, half):
        forward_copy(side * half + mate(k), me).start()

    sums_done(1)
    for t, body in ((1, ready_wide(1)), (2, ready_tall)):
        for g in range(len(groups[t])):
            ready(t, g, body)
            send_near(t, g)
    for t in (1, 2):
        own(t, 0, experts)

    for k in range(1, half):
        other = side * half + mate(k)
        router_copy(other, other).wait_recv()
        forward_copy(other, other).wait_recv()
    for k in range(1, owners):
        col_copy(lax.rem(home + k, owners), home).start()

    for d in range(2, chips):
        for t in range(3):
            for g in range(len(groups[t])):
                if t == 0 and d == 2:
                    continue
                send_at(t, g, d)

    for k in range(1, owners):
        other = lax.rem(home + k, owners)
        col_copy(other, other).wait_recv()
        col_copy(other, home).wait_send()
    router_copy(facing, me).wait_send()
    for k in range(1, half):
        other = side * half + mate(k)
        router_copy(other, me).wait_send()
        forward_copy(other, me).wait_send()
        for s in range(2):
            side_copy(s, mate(k), member).wait_send()
            total_copy(s, mate(k), member).wait_send()
    for s in range(2):
        half_copy(s).wait_send()
    for k in range(1, n):
        early_copy(peer(k), me).wait_send()
    for t in range(3):
        for g in range(len(groups[t])):

            @pl.loop(1, n)
            def _(k):
                block_copy(t, g, peer(k), peer(k)).wait_recv()
                block_copy(t, g, peer(k), me).wait_send()


def write_back(count, *refs):
    ins, outs, sem = refs[:count], refs[count : 2 * count], refs[2 * count]
    copies = [
        pltpu.make_async_copy(a, b, sem.at[i]) for i, (a, b) in enumerate(zip(ins, outs))
    ]
    for copy in copies:
        copy.start()
    for copy in copies:
        copy.wait()


def local(n, owners, gate, up, down, router_weight, router_gain):
    experts, rows, width = gate.shape
    share = width // n
    half = n // 2
    pair = 2 * share
    early, groups, _, total_groups = plan(experts)
    slots = min(SLOTS, experts)
    router = router_weight.T
    gain = router_gain.reshape(1, -1)
    columns = router.shape[0]
    anywhere = pl.BlockSpec(memory_space=pl.ANY)
    vmem = pl.BlockSpec(memory_space=pltpu.VMEM)
    hbm = pl.BlockSpec(memory_space=pltpu.HBM)
    f32, bf16 = jnp.float32, jnp.bfloat16
    dma = pltpu.SemaphoreType.DMA
    shapes = (
        ((experts, rows * n, share), bf16),
        ((experts, rows * n, share), bf16),
        ((experts, share, rows * n), bf16),
        ((experts, share), f32),
        ((experts, share), f32),
        ((experts, share), f32),
        ((owners, columns, rows * n), bf16),
    )
    results = pl.pallas_call(
        functools.partial(exchange, n, owners),
        name="exchange",
        out_shape=tuple(pltpu.VMEM(*s) for s in shapes),
        in_specs=[anywhere] * 5,
        out_specs=(vmem,) * len(shapes),
        scratch_shapes=[
            pltpu.VMEM((early, rows, width), f32),
            pltpu.VMEM((slots, rows, width), f32),
            pltpu.VMEM((slots, width, rows), f32),
            pltpu.VMEM((2, n, experts, rows, share), bf16),
            pltpu.VMEM((n, experts, share, rows), bf16),
            pltpu.VMEM((2, early, width // 2), f32),
            pltpu.VMEM((n, early, width // 2), f32),
            pltpu.VMEM((early, width // 2), f32),
            pltpu.VMEM((half, 3, experts, pair), f32),
            pltpu.VMEM((half, 3, experts, pair), f32),
            pltpu.VMEM((3, experts, pair), f32),
            pltpu.VMEM((3, experts, pair), f32),
            pltpu.VMEM((half, 3, experts, pair), f32),
            pltpu.VMEM((half, 3, experts, pair), f32),
            pltpu.VMEM((columns, rows), f32),
            pltpu.VMEM((1, rows), f32),
            pltpu.VMEM((columns, rows), bf16),
            dma((4, max(slots, 2, early))),
            dma((n,)),
            dma((n,)),
            dma((2, half)),
            dma((2, half)),
            dma((2,)),
            dma((2,)),
            dma((2, half)),
            dma((2, half)),
            dma((n,)),
            dma((n,)),
            dma((n,)),
            dma((n,)),
            dma((owners,)),
            dma((owners,)),
            dma((total_groups, n)),
            dma((total_groups, n)),
        ],
        compiler_params=pltpu.CompilerParams(
            collective_id=0, has_side_effects=True, vmem_limit_bytes=38 * 1024 * 1024
        ),
    )(gate, up, down, router, gain)
    outs = pl.pallas_call(
        functools.partial(write_back, len(shapes)),
        name="write_back",
        out_shape=tuple(pltpu.HBM(*s) for s in shapes),
        in_specs=[vmem] * len(shapes),
        out_specs=(hbm,) * len(shapes),
        scratch_shapes=[dma((len(shapes),))],
        compiler_params=pltpu.CompilerParams(vmem_limit_bytes=1024 * 1024),
    )(*results)
    serve_router = outs[6].reshape(owners * columns, rows * n).T
    return (*outs[:6], serve_router)


def solution(mesh):
    return jax.shard_map(
        functools.partial(local, mesh.shape["rows"], mesh.shape["owner"]),
        mesh=mesh,
        in_specs=(
            P("owner", "rows", None),
            P("owner", "rows", None),
            P("owner", None, "rows"),
            P("rows", "owner"),
            P("rows"),
        ),
        out_specs=(
            P("owner", None, "rows"),
            P("owner", None, "rows"),
            P("owner", "rows", None),
            P("owner", "rows"),
            P("owner", "rows"),
            P("owner", "rows"),
            P(),
        ),
        check_vma=False,
    )
```

time: 595 us -> 566 us (0.951)
  local copies, waits for them, and re-layouts: 25.7 us -> 0 us
    unnamed x6 -> x0, local copies, waits for them, and re-layouts: 24.4 us -> none
    pallas_call x1, Pallas kernels: 563 us -> 553 us  [local(): pl.pallas_call(functools.partial(exchange, n, owners), name='exchange', o...]
    pallas_call x0 -> x1, Pallas kernels: none -> 8.75 us  [local(): pl.pallas_call(functools.partial(write_back, len(shapes)), name='write_ba...]
where the time goes in v1:
time: 566 us; the launch traced here: 562 us
  Pallas kernels  561 us (99%)
    pallas_call x1, Pallas kernels, local(): pl.pallas_call(functools.partial(exchange, n, owners), name='exchange', o...  553 us

profile of v1, /device:TPU:9, one launch (start us, length us, event | category | flops | bytes accessed | tf_op | source)
XLA Modules:
  0.0 561.9 jit_solution(8320304526471114822)
XLA Ops:
  0.6 552.5 %exchange.1 = (bf16[16,2048,128]{2,1,0:T(8,128)(2,1)S(1)}, bf16[16,2048,128]{2,1,0:T(8,128)(2,1)S(1)}, bf16[16,128,2048]{2,1,0:T(8,128)(2,1)S(1)}, f32[16,128]{1...) custom-call(f32[16,256,1024]{2,1,0:T(8,128)} %gate.1, ...), custom_call_target="tpu_custom_call" | custom-call | tf_op jit(solution)/shard_map/exchange/pallas_call | solution.py:523
  553.2 8.8 %write_back.1 = (bf16[16,2048,128]{2,1,0:T(8,128)(2,1)}, bf16[16,2048,128]{2,1,0:T(8,128)(2,1)}, bf16[16,128,2048]{2,1,0:T(8,128)(2,1)}, f32[16,128]{1,0:T(8,128...) custom-call(bf16[16,2048,128]{2,1,0:T(8,128)(2,1)S(1)} %get-tuple-element.21.refs_0_, ...), custom_call_target="tpu_custom_call" | custom-call | tf_op jit(solution)/shard_map/write_back/pallas_call | solution.py:569

commit v2 on v1

--- a/solution.py
+++ b/solution.py
@@ -10,6 +10,8 @@
 CORES = 2
 SLOTS = 4
 EARLY = 2
+SHADOW = 6
+CHUNKS = 4
 GROUPS = 4
 MESH = pl.DeviceIdType.MESH
 
@@ -130,24 +132,21 @@
     for e in range(early):
         load_first(e).start()
 
-    def fill(t, start):
-        for e in range(start, min(start + slots, experts)):
+    def fill(t, start, stop):
+        for e in range(start, min(start + slots, stop)):
             load(t, e).start()
 
-    def take(t, e, body):
-        load(t, e).wait()
-        body(e, lax.rem(e, slots))
-
-        @pl.when(e + slots < experts)
-        def _():
-            load(t, e + slots).start()
-
-    def run(t, start, stop, body):
+    def run(t, start, stop, last, body):
         @pl.loop(start, stop)
         def _(e):
-            take(t, e, body)
-
-    fill(0, early)
+            load(t, e).wait()
+            body(e, lax.rem(e, slots))
+
+            @pl.when(e + slots < last)
+            def _():
+                load(t, e + slots).start()
+
+    fill(0, early, experts)
     weight_load = pltpu.make_async_copy(router_weight, weight, load_sem.at[3, 0])
     gain_load = pltpu.make_async_copy(router_gain, gain, load_sem.at[3, 1])
     weight_load.start()
@@ -200,7 +199,37 @@
     for k in range(1, n):
         early_copy(peer(k), me).start()
 
-    run(0, early, experts, sums_wide(0))
+    weight_load.wait()
+    gain_load.wait()
+    router[...] = (weight[...] * gain[...]).astype(jnp.bfloat16)
+    out_router[home, :, span] = router[...]
+
+    def strip(src):
+        return out_router.at[home, :, pl.ds(pl.multiple_of(src * rows, rows), rows)]
+
+    def router_copy(to, src):
+        return remote(router, strip(src), router_send.at[to], router_recv.at[src], rows=to)
+
+    def forward_copy(to, src):
+        return remote(
+            strip(lax.rem(src + half, n)),
+            strip(lax.rem(src + half, n)),
+            fwd_send.at[to],
+            fwd_recv.at[src],
+            rows=to,
+        )
+
+    def col_copy(to, src):
+        return remote(
+            out_router.at[src], out_router.at[src], col_send.at[to], col_recv.at[src], owner=to
+        )
+
+    for k in range(1, half):
+        router_copy(side * half + mate(k), me).start()
+    router_copy(facing, me).start()
+
+    shadow = min(early + SHADOW, experts)
+    run(0, early, shadow, experts, sums_wide(0))
 
     stages = (pl.ds(0, 1), pl.ds(1, 2))
 
@@ -256,8 +285,6 @@
                 inverse[q, t] = 1.0 / (total[q, t] / count)
             mine = total[me // 2, t] / count
             scales[t][...] = jnp.where(lax.rem(me, 2) == 0, mine[:, :share], mine[:, share:])
-
-    sums_side(0)
 
     def block_copy(t, g, to, src):
         start, size = groups[t][g]
@@ -293,9 +320,14 @@
         for c in range(1, CORES):
             block_copy(t, g, chip * CORES + lax.rem(core + c, CORES), me).start()
 
-    def send_across(g, k):
-        there = jnp.where(side == 0, half_chips + k, half_chips - 1 - k)
-        send_chip(0, g, there)
+    inner = (chip == half_chips - 1) | (chip == half_chips)
+
+    def send_across(who, pieces):
+        @pl.when(who)
+        def _():
+            for g, k in pieces:
+                there = jnp.where(side == 0, half_chips + k, half_chips - 1 - k)
+                send_chip(0, g, there)
 
     def scaled_pair(t, e, q, block, factor):
         value = (block * factor).astype(jnp.bfloat16)
@@ -344,9 +376,9 @@
             else:
                 out_down[e, :, span] = send_tall[me, e]
 
-    def ready(t, g, body):
+    def ready(t, g, last, body):
         start, size = groups[t][g]
-        run(t, start, start + size, body)
+        run(t, start, start + size, last, body)
 
     acc = early_part[1 - side]
     for k in range(1, n):
@@ -354,94 +386,73 @@
         acc = acc + early_got[peer(k)]
     early_inv[...] = 1.0 / (acc / count)
 
-    fill(1, 0)
+    pieces = [(e, k) for e in range(early) for k in range(half_chips)]
+    cut = max(1, len(pieces) // 4)
+    middle = experts // 2
+    rest = range(early, len(groups[0]))
+    low = [g for g in rest if groups[0][g][0] < middle]
+    high = [g for g in rest if groups[0][g][0] >= middle]
+
     half_first(0, 1 - side, early_factor(0))
-    send_across(0, 0)
-    sums_across(0)
-    for k in range(1, half_chips):
-        send_across(0, k)
+    send_across(inner, pieces[:cut])
+    run(0, shadow, experts, experts, sums_wide(0))
+    fill(1, 0, middle)
+    sums_side(0)
     for e in range(1, early):
         half_first(e, 1 - side, early_factor(e))
-    run(1, 0, experts, sums_wide(1))
-    fill(0, early)
+    send_across(inner, pieces[cut : 2 * cut])
+    sums_across(0)
+    send_across(inner, pieces[2 * cut : 3 * cut])
+    run(1, 0, middle, middle, sums_wide(1))
+    fill(0, early, middle)
+    fill(2, 0, experts)
     sums_back(0)
-    for e in range(1, early):
-        for k in range(half_chips):
-            send_across(e, k)
-
-    weight_load.wait()
-    gain_load.wait()
-    router[...] = (weight[...] * gain[...]).astype(jnp.bfloat16)
-    out_router[home, :, span] = router[...]
-
-    def strip(src):
-        return out_router.at[home, :, pl.ds(pl.multiple_of(src * rows, rows), rows)]
-
-    def router_copy(to, src):
-        return remote(router, strip(src), router_send.at[to], router_recv.at[src], rows=to)
-
-    def forward_copy(to, src):
-        return remote(
-            strip(lax.rem(src + half, n)),
-            strip(lax.rem(src + half, n)),
-            fwd_send.at[to],
-            fwd_recv.at[src],
-            rows=to,
-        )
-
-    def col_copy(to, src):
-        return remote(
-            out_router.at[src], out_router.at[src], col_send.at[to], col_recv.at[src], owner=to
-        )
-
-    for k in range(1, half):
-        router_copy(side * half + mate(k), me).start()
-    router_copy(facing, me).start()
-
+    send_across(inner, pieces[3 * cut :])
+    send_across(jnp.logical_not(inner), pieces)
     sums_done(0)
 
+    for g in low:
+        ready(0, g, middle, ready_wide(0))
+        send_near(0, g)
+    fill(1, middle, experts)
     for e in range(early):
         half_first(e, side, lambda p, q: inverse[q, 0, pl.ds(e, 1), :])
     for g in range(early):
         send_near(0, g)
-    rest = range(early, len(groups[0]))
-    for g in rest:
-        ready(0, g, ready_wide(0))
+    run(1, middle, experts, experts, sums_wide(1))
+    fill(0, middle, experts)
+    run(2, 0, experts, experts, sums_tall)
+    fill(2, 0, experts)
+    sums_side(1)
+    for g in high[:1]:
+        ready(0, g, experts, ready_wide(0))
         send_near(0, g)
-    fill(2, 0)
+    sums_across(1)
+    for g in high[1:]:
+        ready(0, g, experts, ready_wide(0))
+        send_near(0, g)
+    fill(1, 0, experts)
+    sums_back(1)
+
+    def send_far(t, g):
+        for d in range(2, chips):
+            send_at(t, g, d)
+
+    for g in low:
+        send_far(0, g)
     own(0, 0, experts)
-    run(2, 0, experts, sums_tall)
-    fill(1, 0)
-    fill(2, 0)
-
-    def spread(t, g, d):
-        send_at(t, g, d)
-
-    def two(g):
-        if chips > 2:
-            send_at(0, g, 2)
-
-    cuts = [list(rest)[:1], list(rest)[1:2], list(rest)[2:]]
-    sums_side(1)
-    for g in range(early):
-        two(g)
-    for g in cuts[0]:
-        two(g)
-    sums_across(1)
-    for g in cuts[1]:
-        two(g)
-    sums_back(1)
-    for g in cuts[2]:
-        two(g)
-
     router_copy(facing, facing).wait_recv()
     for k in range(1, half):
         forward_copy(side * half + mate(k), me).start()
-
     sums_done(1)
+    for g in [*range(early), *high]:
+        send_far(0, g)
     for t, body in ((1, ready_wide(1)), (2, ready_tall)):
         for g in range(len(groups[t])):
-            ready(t, g, body)
+            ready(t, g, experts, body)
+            send_far(t, g)
+    for t in (1, 2):
+        for g in range(len(groups[t])):
             send_near(t, g)
     for t in (1, 2):
         own(t, 0, experts)
@@ -452,13 +463,6 @@
         forward_copy(other, other).wait_recv()
     for k in range(1, owners):
         col_copy(lax.rem(home + k, owners), home).start()
-
-    for d in range(2, chips):
-        for t in range(3):
-            for g in range(len(groups[t])):
-                if t == 0 and d == 2:
-                    continue
-                send_at(t, g, d)
 
     for k in range(1, owners):
         other = lax.rem(home + k, owners)
@@ -485,11 +489,18 @@
                 block_copy(t, g, peer(k), me).wait_send()
 
 
+def chunks_of(shape):
+    count = CHUNKS if len(shape) == 3 and shape[0] % CHUNKS == 0 else 1
+    size = shape[0] // count
+    return [pl.ds(i * size, size) for i in range(count)]
+
+
 def write_back(count, *refs):
     ins, outs, sem = refs[:count], refs[count : 2 * count], refs[2 * count]
-    copies = [
-        pltpu.make_async_copy(a, b, sem.at[i]) for i, (a, b) in enumerate(zip(ins, outs))
-    ]
+    copies = []
+    for i, (a, b) in enumerate(zip(ins, outs)):
+        for j, some in enumerate(chunks_of(a.shape)):
+            copies.append(pltpu.make_async_copy(a.at[some], b.at[some], sem.at[i, j]))
     for copy in copies:
         copy.start()
     for copy in copies:
@@ -572,7 +583,7 @@
         out_shape=tuple(pltpu.HBM(*s) for s in shapes),
         in_specs=[vmem] * len(shapes),
         out_specs=(hbm,) * len(shapes),
-        scratch_shapes=[dma((len(shapes),))],
+        scratch_shapes=[dma((len(shapes), CHUNKS))],
         compiler_params=pltpu.CompilerParams(vmem_limit_bytes=1024 * 1024),
     )(*results)
     serve_router = outs[6].reshape(owners * columns, rows * n).T

time: 566 us -> 563 us (level)
  no operation moved by 1% of the time
where the time goes in v2:
time: 563 us
  Pallas kernels  562 us (100%)
    pallas_call x1, Pallas kernels, local(): pl.pallas_call(functools.partial(exchange, n, owners), name='exchange', o...  554 us

profile of v2, /device:TPU:9, one launch (start us, length us, event | category | flops | bytes accessed | tf_op | source)
XLA Modules:
  0.0 562.9 jit_solution(5795440914626306501)
XLA Ops:
  0.6 553.7 %exchange.1 = (bf16[16,2048,128]{2,1,0:T(8,128)(2,1)S(1)}, bf16[16,2048,128]{2,1,0:T(8,128)(2,1)S(1)}, bf16[16,128,2048]{2,1,0:T(8,128)(2,1)S(1)}, f32[16,128]{1...) custom-call(f32[16,256,1024]{2,1,0:T(8,128)} %gate.1, ...), custom_call_target="tpu_custom_call" | custom-call | tf_op jit(solution)/shard_map/exchange/pallas_call | solution.py:534
  554.3 8.6 %write_back.1 = (bf16[16,2048,128]{2,1,0:T(8,128)(2,1)}, bf16[16,2048,128]{2,1,0:T(8,128)(2,1)}, bf16[16,128,2048]{2,1,0:T(8,128)(2,1)}, f32[16,128]{1,0:T(8,128...) custom-call(bf16[16,2048,128]{2,1,0:T(8,128)(2,1)S(1)} %get-tuple-element.21.refs_0_, ...), custom_call_target="tpu_custom_call" | custom-call | tf_op jit(solution)/shard_map/write_back/pallas_call | solution.py:580

commit v3 on v2

--- a/solution.py
+++ b/solution.py
@@ -32,6 +32,13 @@
     groups = [groups_of(experts, early), groups_of(experts, 0), groups_of(experts, 0)]
     base = [0, len(groups[0]), len(groups[0]) + len(groups[1])]
     return early, groups, base, sum(len(g) for g in groups)
+
+
+def sides(n, me):
+    chips = n // CORES
+    chip = me // CORES
+    inner = (chip == chips // 2 - 1) | (chip == chips // 2)
+    return chip, inner, jnp.where(chip < chips // 2, chips // 2, chips // 2 - 1)
 
 
 def exchange(
@@ -49,6 +56,7 @@
     scale_up,
     scale_down,
     out_router,
+    late_send,
     first,
     wide,
     tall,
@@ -93,7 +101,7 @@
     slots = wide.shape[0]
     chips = n // CORES
     half_chips = chips // 2
-    chip = me // CORES
+    chip, inner, across = sides(n, me)
     core = lax.rem(me, CORES)
     side = me // half
     member = lax.rem(me, half)
@@ -303,31 +311,26 @@
         for c in range(CORES):
             block_copy(t, g, there * CORES + lax.rem(core + c, CORES), me).start()
 
-    def send_at(t, g, d):
-        first_ones = t == 0 and g < early
-        for way in (1, -1):
-            there = chip + way * d
-            ok = (there >= 0) & (there < chips)
-            if first_ones:
-                ok = ok & (there // half_chips == chip // half_chips)
-
-            @pl.when(ok)
-            def _():
-                send_chip(t, g, there)
-
-    def send_near(t, g):
-        send_at(t, g, 1)
+    def send_side(t, g):
+        for d in range(1, half_chips):
+            for way in (1, -1):
+                there = chip + way * d
+
+                @pl.when((there // half_chips == chip // half_chips) & (there >= 0))
+                def _():
+                    send_chip(t, g, there)
+
         for c in range(1, CORES):
             block_copy(t, g, chip * CORES + lax.rem(core + c, CORES), me).start()
 
-    inner = (chip == half_chips - 1) | (chip == half_chips)
+    last = (2, len(groups[2]) - 1)
 
     def send_across(who, pieces):
         @pl.when(who)
         def _():
-            for g, k in pieces:
+            for t, g, k in pieces:
                 there = jnp.where(side == 0, half_chips + k, half_chips - 1 - k)
-                send_chip(0, g, there)
+                send_chip(t, g, there)
 
     def scaled_pair(t, e, q, block, factor):
         value = (block * factor).astype(jnp.bfloat16)
@@ -386,7 +389,8 @@
         acc = acc + early_got[peer(k)]
     early_inv[...] = 1.0 / (acc / count)
 
-    pieces = [(e, k) for e in range(early) for k in range(half_chips)]
+    pieces = [(0, e, k) for e in range(early) for k in range(half_chips)]
+    outer = jnp.logical_not(inner)
     cut = max(1, len(pieces) // 4)
     middle = experts // 2
     rest = range(early, len(groups[0]))
@@ -408,52 +412,48 @@
     fill(2, 0, experts)
     sums_back(0)
     send_across(inner, pieces[3 * cut :])
-    send_across(jnp.logical_not(inner), pieces)
+    send_across(outer, pieces)
     sums_done(0)
 
+    def next_group(g, stop):
+        ready(0, g, stop, ready_wide(0))
+        send_across(inner, [(0, g, 0)])
+        send_side(0, g)
+
     for g in low:
-        ready(0, g, middle, ready_wide(0))
-        send_near(0, g)
+        next_group(g, middle)
     fill(1, middle, experts)
     for e in range(early):
         half_first(e, side, lambda p, q: inverse[q, 0, pl.ds(e, 1), :])
     for g in range(early):
-        send_near(0, g)
+        send_side(0, g)
     run(1, middle, experts, experts, sums_wide(1))
     fill(0, middle, experts)
     run(2, 0, experts, experts, sums_tall)
     fill(2, 0, experts)
     sums_side(1)
     for g in high[:1]:
-        ready(0, g, experts, ready_wide(0))
-        send_near(0, g)
+        next_group(g, experts)
     sums_across(1)
     for g in high[1:]:
-        ready(0, g, experts, ready_wide(0))
-        send_near(0, g)
+        next_group(g, experts)
     fill(1, 0, experts)
     sums_back(1)
-
-    def send_far(t, g):
-        for d in range(2, chips):
-            send_at(t, g, d)
-
-    for g in low:
-        send_far(0, g)
+    send_across(inner, [(0, g, k) for g in low for k in range(1, half_chips)])
     own(0, 0, experts)
     router_copy(facing, facing).wait_recv()
     for k in range(1, half):
         forward_copy(side * half + mate(k), me).start()
     sums_done(1)
-    for g in [*range(early), *high]:
-        send_far(0, g)
+    send_across(inner, [(0, g, k) for g in high for k in range(1, half_chips)])
     for t, body in ((1, ready_wide(1)), (2, ready_tall)):
         for g in range(len(groups[t])):
             ready(t, g, experts, body)
-            send_far(t, g)
-    for t in (1, 2):
-        for g in range(len(groups[t])):
-            send_near(t, g)
+            send_across(inner, [(t, g, k) for k in range(half_chips) if (t, g, k) != (*last, 0)])
+            send_side(t, g)
+    start, size = groups[2][-1]
+    for c in range(CORES):
+        late_send[c] = send_tall[across * CORES + c, pl.ds(start, size)]
     for t in (1, 2):
         own(t, 0, experts)
 
@@ -463,6 +463,21 @@
         forward_copy(other, other).wait_recv()
     for k in range(1, owners):
         col_copy(lax.rem(home + k, owners), home).start()
+
+    @pl.when(outer)
+    def _():
+        for c in range(CORES):
+            block_copy(*last, across * CORES + c, across * CORES + c).wait_recv()
+
+    for k in range(half_chips):
+        send_across(
+            outer,
+            [
+                (t, g, k)
+                for t in range(3)
+                for g in range(early if t == 0 else 0, len(groups[t]))
+            ],
+        )
 
     for k in range(1, owners):
         other = lax.rem(home + k, owners)
@@ -485,8 +500,72 @@
 
             @pl.loop(1, n)
             def _(k):
-                block_copy(t, g, peer(k), peer(k)).wait_recv()
-                block_copy(t, g, peer(k), me).wait_send()
+                other = peer(k)
+                if (t, g) != last:
+                    block_copy(t, g, other, other).wait_recv()
+                    block_copy(t, g, other, me).wait_send()
+                else:
+                    facing_chip = other // CORES == across
+
+                    @pl.when(jnp.logical_not(facing_chip))
+                    def _():
+                        block_copy(t, g, other, other).wait_recv()
+
+                    @pl.when(jnp.logical_not(facing_chip & inner))
+                    def _():
+                        block_copy(t, g, other, me).wait_send()
+
+
+def late_exchange(n, late_send, _, late_got, send_sem, recv_sem):
+    me = lax.axis_index("rows")
+    _, inner, across = sides(n, me)
+    core = lax.rem(me, CORES)
+
+    def copy(to, src):
+        return pltpu.make_async_remote_copy(
+            src_ref=late_send.at[to],
+            dst_ref=late_got.at[src],
+            send_sem=send_sem.at[to],
+            recv_sem=recv_sem.at[src],
+            device_id={"rows": across * CORES + to},
+            device_id_type=MESH,
+        )
+
+    @pl.when(inner)
+    def _():
+        barrier = pltpu.get_barrier_semaphore()
+        for c in range(CORES):
+            pl.semaphore_signal(
+                barrier, inc=1, device_id={"rows": across * CORES + c}, device_id_type=MESH
+            )
+        pl.semaphore_wait(barrier, CORES)
+        for c in range(CORES):
+            copy(lax.rem(core + c, CORES), core).start()
+        for c in range(CORES):
+            copy(c, c).wait_recv()
+            copy(c, core).wait_send()
+
+
+def late_place(n, start, late_got, down, out, sem):
+    me = lax.axis_index("rows")
+    _, inner, across = sides(n, me)
+    size, rows = late_got.shape[1], late_got.shape[3]
+
+    @pl.when(inner)
+    def _():
+        copies = []
+        for c in range(CORES):
+            src = across * CORES + c
+            at = pl.ds(pl.multiple_of(src * rows, rows), rows)
+            copies.append(
+                pltpu.make_async_copy(
+                    late_got.at[c], out.at[pl.ds(start, size), :, at], sem.at[c]
+                )
+            )
+        for copy in copies:
+            copy.start()
+        for copy in copies:
+            copy.wait()
 
 
 def chunks_of(shape):
@@ -531,12 +610,14 @@
         ((experts, share), f32),
         ((owners, columns, rows * n), bf16),
     )
-    results = pl.pallas_call(
+    start, size = groups[2][-1]
+    late = ((CORES, size, share, rows), bf16)
+    *results, late_send = pl.pallas_call(
         functools.partial(exchange, n, owners),
         name="exchange",
-        out_shape=tuple(pltpu.VMEM(*s) for s in shapes),
+        out_shape=tuple(pltpu.VMEM(*s) for s in (*shapes, late)),
         in_specs=[anywhere] * 5,
-        out_specs=(vmem,) * len(shapes),
+        out_specs=(vmem,) * (len(shapes) + 1),
         scratch_shapes=[
             pltpu.VMEM((early, rows, width), f32),
             pltpu.VMEM((slots, rows, width), f32),
@@ -586,8 +667,29 @@
         scratch_shapes=[dma((len(shapes), CHUNKS))],
         compiler_params=pltpu.CompilerParams(vmem_limit_bytes=1024 * 1024),
     )(*results)
+    late_got = pl.pallas_call(
+        functools.partial(late_exchange, n),
+        name="late_exchange",
+        out_shape=pltpu.VMEM(*late),
+        in_specs=[vmem, anywhere],
+        out_specs=vmem,
+        scratch_shapes=[dma((CORES,)), dma((CORES,))],
+        compiler_params=pltpu.CompilerParams(
+            collective_id=1, has_side_effects=True, vmem_limit_bytes=1024 * 1024
+        ),
+    )(late_send, outs[3])
+    ready_down = pl.pallas_call(
+        functools.partial(late_place, n, start),
+        name="late_place",
+        out_shape=pltpu.HBM(*shapes[2]),
+        in_specs=[vmem, hbm],
+        out_specs=hbm,
+        scratch_shapes=[dma((CORES,))],
+        input_output_aliases={1: 0},
+        compiler_params=pltpu.CompilerParams(vmem_limit_bytes=1024 * 1024),
+    )(late_got, outs[2])
     serve_router = outs[6].reshape(owners * columns, rows * n).T
-    return (*outs[:6], serve_router)
+    return (*outs[:2], ready_down, *outs[3:6], serve_router)
 
 
 def solution(mesh):

time: 563 us -> 558 us (level)
  Pallas kernels: 562 us -> 554 us
    pallas_call x1, Pallas kernels: 554 us -> 416 us  [local(): pl.pallas_call(functools.partial(exchange, n, owners), name='exchange', o...]
    pallas_call x0 -> x2, Pallas kernels: none -> 129 us  [the longest x1 128 us: local(): pl.pallas_call(functools.partial(late_exchange, n), name='late_exchange',...]
where the time goes in v3:
time: 558 us; the launch traced here: 555 us
  Pallas kernels  554 us (99%)
    pallas_call x1, Pallas kernels, local(): pl.pallas_call(functools.partial(exchange, n, owners), name='exchange', o...  416 us
    pallas_call x1, Pallas kernels, local(): pl.pallas_call(functools.partial(late_exchange, n), name='late_exchange',...  128 us

profile of v3, /device:TPU:9, one launch (start us, length us, event | category | flops | bytes accessed | tf_op | source)
XLA Modules:
  0.0 555.1 jit_solution(8115987993682877655)
XLA Ops:
  0.6 416.3 %exchange.1 = (bf16[16,2048,128]{2,1,0:T(8,128)(2,1)S(1)}, bf16[16,2048,128]{2,1,0:T(8,128)(2,1)S(1)}, bf16[16,128,2048]{2,1,0:T(8,128)(2,1)S(1)}, f32[16,128]{1...) custom-call(f32[16,256,1024]{2,1,0:T(8,128)} %gate.1, ...), custom_call_target="tpu_custom_call" | custom-call | tf_op jit(solution)/shard_map/exchange/pallas_call | solution.py:615
  416.9 8.6 %write_back.1 = (bf16[16,2048,128]{2,1,0:T(8,128)(2,1)}, bf16[16,2048,128]{2,1,0:T(8,128)(2,1)}, bf16[16,128,2048]{2,1,0:T(8,128)(2,1)}, f32[16,128]{1,0:T(8,128...) custom-call(bf16[16,2048,128]{2,1,0:T(8,128)(2,1)S(1)} %get-tuple-element.22.refs_0_, ...), custom_call_target="tpu_custom_call" | custom-call | tf_op jit(solution)/shard_map/write_back/pallas_call | solution.py:661
  425.6 0.0 copy-start
  425.6 0.7 copy-done
  426.3 128.0 %late_exchange.1.late_got = bf16[2,4,128,256]{3,2,1,0:T(8,128)(2,1)S(1)} custom-call(bf16[2,4,128,256]{3,2,1,0:T(8,128)(2,1)S(1)} %get-tuple-element.31.late_send, f32[16,128]{1,0:T(8,128)S(1)} %copy-done), custom_call_target="tpu_custom_call" | custom-call | tf_op jit(solution)/shard_map/late_exchange/pallas_call | solution.py:670
  554.3 0.8 late_place.1
Async XLA Ops:
  425.6 0.7 copy-start

commit v4 on v3

--- a/solution.py
+++ b/solution.py
@@ -9,7 +9,7 @@
 
 CORES = 2
 SLOTS = 4
-EARLY = 2
+EARLY = 3
 SHADOW = 6
 CHUNKS = 4
 GROUPS = 4
@@ -28,8 +28,10 @@
 
 
 def plan(experts):
-    early = min(EARLY, experts // 2)
+    early = max(1, min(EARLY, experts // 4))
     groups = [groups_of(experts, early), groups_of(experts, 0), groups_of(experts, 0)]
+    (start, size), (_, more) = groups[2][-2:]
+    groups[2][-2:] = [(start, size + more)]
     base = [0, len(groups[0]), len(groups[0]) + len(groups[1])]
     return early, groups, base, sum(len(g) for g in groups)
 
@@ -195,6 +197,9 @@
 
     pl.semaphore_wait(barrier, n - 1 + owners - 1)
 
+    inners = (half_chips - 1, half_chips)
+    reach = [c * CORES + i for c in inners for i in range(CORES)]
+
     def early_copy(to, src):
         return remote(
             early_part.at[1 - to // half],
@@ -204,8 +209,11 @@
             rows=to,
         )
 
-    for k in range(1, n):
-        early_copy(peer(k), me).start()
+    for to in reach:
+
+        @pl.when(me != to)
+        def _():
+            early_copy(to, me).start()
 
     weight_load.wait()
     gain_load.wait()
@@ -324,6 +332,11 @@
             block_copy(t, g, chip * CORES + lax.rem(core + c, CORES), me).start()
 
     last = (2, len(groups[2]) - 1)
+    held, want = [], groups[2][-1][1] - 1
+    for g in reversed(range(len(groups[0]))):
+        if groups[0][g][1] <= want:
+            held.append(g)
+            want -= groups[0][g][1]
 
     def send_across(who, pieces):
         @pl.when(who)
@@ -345,6 +358,9 @@
 
     def early_factor(e):
         return lambda p, q: early_inv[pl.ds(e, 1), p * pair : (p + 1) * pair]
+
+    def late_factor(e):
+        return lambda p, q: inverse[q, 0, pl.ds(e, 1), :]
 
     def ready_wide(t):
         def body(e, slot):
@@ -383,11 +399,13 @@
         start, size = groups[t][g]
         run(t, start, start + size, last, body)
 
-    acc = early_part[1 - side]
-    for k in range(1, n):
-        early_copy(peer(k), peer(k)).wait_recv()
-        acc = acc + early_got[peer(k)]
-    early_inv[...] = 1.0 / (acc / count)
+    @pl.when(inner)
+    def _():
+        acc = early_part[1 - side]
+        for k in range(1, n):
+            early_copy(peer(k), peer(k)).wait_recv()
+            acc = acc + early_got[peer(k)]
+        early_inv[...] = 1.0 / (acc / count)
 
     pieces = [(0, e, k) for e in range(early) for k in range(half_chips)]
     outer = jnp.logical_not(inner)
@@ -397,13 +415,18 @@
     low = [g for g in rest if groups[0][g][0] < middle]
     high = [g for g in rest if groups[0][g][0] >= middle]
 
-    half_first(0, 1 - side, early_factor(0))
+    def early_ready(e):
+        @pl.when(inner)
+        def _():
+            half_first(e, 1 - side, early_factor(e))
+
+    early_ready(0)
     send_across(inner, pieces[:cut])
     run(0, shadow, experts, experts, sums_wide(0))
     fill(1, 0, middle)
     sums_side(0)
     for e in range(1, early):
-        half_first(e, 1 - side, early_factor(e))
+        early_ready(e)
     send_across(inner, pieces[cut : 2 * cut])
     sums_across(0)
     send_across(inner, pieces[2 * cut : 3 * cut])
@@ -412,21 +435,34 @@
     fill(2, 0, experts)
     sums_back(0)
     send_across(inner, pieces[3 * cut :])
-    send_across(outer, pieces)
     sums_done(0)
+
+    def send_gate_side(g):
+        if g in held:
+
+            @pl.when(inner)
+            def _():
+                send_side(0, g)
+        else:
+            send_side(0, g)
 
     def next_group(g, stop):
         ready(0, g, stop, ready_wide(0))
         send_across(inner, [(0, g, 0)])
-        send_side(0, g)
+        send_gate_side(g)
 
     for g in low:
         next_group(g, middle)
     fill(1, middle, experts)
     for e in range(early):
-        half_first(e, side, lambda p, q: inverse[q, 0, pl.ds(e, 1), :])
+        half_first(e, side, late_factor(e))
+
+        @pl.when(outer)
+        def _():
+            half_first(e, 1 - side, late_factor(e))
+
     for g in range(early):
-        send_side(0, g)
+        send_gate_side(g)
     run(1, middle, experts, experts, sums_wide(1))
     fill(0, middle, experts)
     run(2, 0, experts, experts, sums_tall)
@@ -451,6 +487,7 @@
             ready(t, g, experts, body)
             send_across(inner, [(t, g, k) for k in range(half_chips) if (t, g, k) != (*last, 0)])
             send_side(t, g)
+
     start, size = groups[2][-1]
     for c in range(CORES):
         late_send[c] = send_tall[across * CORES + c, pl.ds(start, size)]
@@ -464,20 +501,17 @@
     for k in range(1, owners):
         col_copy(lax.rem(home + k, owners), home).start()
 
+    before = (2, last[1] - 1)
+
     @pl.when(outer)
     def _():
         for c in range(CORES):
-            block_copy(*last, across * CORES + c, across * CORES + c).wait_recv()
+            block_copy(*before, across * CORES + c, across * CORES + c).wait_recv()
+        for g in held:
+            send_side(0, g)
 
     for k in range(half_chips):
-        send_across(
-            outer,
-            [
-                (t, g, k)
-                for t in range(3)
-                for g in range(early if t == 0 else 0, len(groups[t]))
-            ],
-        )
+        send_across(outer, [(t, g, k) for t in range(3) for g in range(len(groups[t]))])
 
     for k in range(1, owners):
         other = lax.rem(home + k, owners)
@@ -493,27 +527,35 @@
             total_copy(s, mate(k), member).wait_send()
     for s in range(2):
         half_copy(s).wait_send()
-    for k in range(1, n):
-        early_copy(peer(k), me).wait_send()
+    for to in reach:
+
+        @pl.when(me != to)
+        def _():
+            early_copy(to, me).wait_send()
+
     for t in range(3):
         for g in range(len(groups[t])):
 
             @pl.loop(1, n)
             def _(k):
                 other = peer(k)
-                if (t, g) != last:
+                facing_chip = other // CORES == across
+                if (t, g) == before:
+
+                    @pl.when(jnp.logical_not(facing_chip & outer))
+                    def _():
+                        block_copy(t, g, other, other).wait_recv()
+
+                    block_copy(t, g, other, me).wait_send()
+                elif (t, g) == last:
+
+                    @pl.when(jnp.logical_not(facing_chip & inner))
+                    def _():
+                        block_copy(t, g, other, other).wait_recv()
+                        block_copy(t, g, other, me).wait_send()
+                else:
                     block_copy(t, g, other, other).wait_recv()
                     block_copy(t, g, other, me).wait_send()
-                else:
-                    facing_chip = other // CORES == across
-
-                    @pl.when(jnp.logical_not(facing_chip))
-                    def _():
-                        block_copy(t, g, other, other).wait_recv()
-
-                    @pl.when(jnp.logical_not(facing_chip & inner))
-                    def _():
-                        block_copy(t, g, other, me).wait_send()
 
 
 def late_exchange(n, late_send, _, late_got, send_sem, recv_sem):

time: 558 us -> 553 us (level)
    pallas_call x1, Pallas kernels: 416 us -> 396 us  [local(): pl.pallas_call(functools.partial(exchange, n, owners), name='exchange', o...]
    pallas_call x1, Pallas kernels: 128 us -> 145 us  [local(): pl.pallas_call(functools.partial(late_exchange, n), name='late_exchange',...]
where the time goes in v4:
time: 553 us
  Pallas kernels  551 us (100%)
    pallas_call x1, Pallas kernels, local(): pl.pallas_call(functools.partial(exchange, n, owners), name='exchange', o...  396 us
    pallas_call x1, Pallas kernels, local(): pl.pallas_call(functools.partial(late_exchange, n), name='late_exchange',...  145 us

profile of v4, /device:TPU:9, one launch (start us, length us, event | category | flops | bytes accessed | tf_op | source)
XLA Modules:
  0.0 552.6 jit_solution(15327128921769542775)
XLA Ops:
  0.6 396.4 %exchange.1 = (bf16[16,2048,128]{2,1,0:T(8,128)(2,1)S(1)}, bf16[16,2048,128]{2,1,0:T(8,128)(2,1)S(1)}, bf16[16,128,2048]{2,1,0:T(8,128)(2,1)S(1)}, f32[16,128]{1...) custom-call(f32[16,256,1024]{2,1,0:T(8,128)} %gate.1, ...), custom_call_target="tpu_custom_call" | custom-call | tf_op jit(solution)/shard_map/exchange/pallas_call | solution.py:657
  397.0 8.6 %write_back.1 = (bf16[16,2048,128]{2,1,0:T(8,128)(2,1)}, bf16[16,2048,128]{2,1,0:T(8,128)(2,1)}, bf16[16,128,2048]{2,1,0:T(8,128)(2,1)}, f32[16,128]{1,0:T(8,128...) custom-call(bf16[16,2048,128]{2,1,0:T(8,128)(2,1)S(1)} %get-tuple-element.22.refs_0_, ...), custom_call_target="tpu_custom_call" | custom-call | tf_op jit(solution)/shard_map/write_back/pallas_call | solution.py:703
  405.7 0.0 copy-start
  405.7 0.7 copy-done
  406.4 145.2 %late_exchange.1.late_got = bf16[2,8,128,256]{3,2,1,0:T(8,128)(2,1)S(1)} custom-call(bf16[2,8,128,256]{3,2,1,0:T(8,128)(2,1)S(1)} %get-tuple-element.31.late_send, f32[16,128]{1,0:T(8,128)S(1)} %copy-done), custom_call_target="tpu_custom_call" | custom-call | tf_op jit(solution)/shard_map/late_exchange/pallas_call | solution.py:712
  551.6 1.0 late_place.1
Async XLA Ops:
  405.7 0.7 copy-start

commit v5 on v4

--- a/solution.py
+++ b/solution.py
@@ -67,6 +67,7 @@
     early_part,
     early_got,
     early_inv,
+    raw_got,
     part,
     got_side,
     half_sum,
@@ -79,6 +80,7 @@
     load_sem,
     early_send,
     early_recv,
+    raw_sem,
     side_send,
     side_recv,
     half_send,
@@ -93,6 +95,7 @@
     col_recv,
     bulk_send,
     bulk_recv,
+    through,
 ):
     me = lax.axis_index("rows")
     home = lax.axis_index("owner")
@@ -193,27 +196,53 @@
         sums = jnp.sum(jnp.abs(first[e]), axis=0, keepdims=True)
         put_part(0, e, sums)
         for s in range(2):
-            early_part[s, pl.ds(e, 1), :] = sums[:, s * (width // 2) : (s + 1) * (width // 2)]
+            early_part[s, e] = sums[:, s * (width // 2) : (s + 1) * (width // 2)]
 
     pl.semaphore_wait(barrier, n - 1 + owners - 1)
 
     inners = (half_chips - 1, half_chips)
     reach = [c * CORES + i for c in inners for i in range(CORES)]
 
-    def early_copy(to, src):
+    early_some = [pl.ds(0, 1)] + [pl.ds(1, early - 1)] * (early > 1)
+
+    def early_copy(i, to, src):
         return remote(
-            early_part.at[1 - to // half],
-            early_got.at[src],
-            early_send.at[to],
-            early_recv.at[src],
+            early_part.at[1 - to // half, early_some[i]],
+            early_got.at[src, early_some[i]],
+            early_send.at[i, to],
+            early_recv.at[i, src],
             rows=to,
         )
 
-    for to in reach:
-
-        @pl.when(me != to)
+    def early_sums(i):
+        for to in reach:
+
+            @pl.when(me != to)
+            def _():
+                early_copy(i, to, me).start()
+
+    early_sums(0)
+
+    raw = share % 128 == 0
+    partner = across * CORES + core
+
+    def raw_copy():
+        return remote(
+            first.at[0, :, pl.ds(pl.multiple_of(partner * share, share), share)],
+            raw_got,
+            raw_sem.at[0],
+            raw_sem.at[1],
+            rows=partner,
+        )
+
+    if raw:
+
+        @pl.when(inner)
         def _():
-            early_copy(to, me).start()
+            raw_copy().start()
+
+    for i in range(1, len(early_some)):
+        early_sums(i)
 
     weight_load.wait()
     gain_load.wait()
@@ -315,8 +344,8 @@
         b = base[t] + g
         return remote(piece, dst, bulk_send.at[b, to], bulk_recv.at[b, src], rows=to)
 
-    def send_chip(t, g, there):
-        for c in range(CORES):
+    def send_chip(t, g, there, cores=range(CORES)):
+        for c in cores:
             block_copy(t, g, there * CORES + lax.rem(core + c, CORES), me).start()
 
     def send_side(t, g):
@@ -332,18 +361,20 @@
             block_copy(t, g, chip * CORES + lax.rem(core + c, CORES), me).start()
 
     last = (2, len(groups[2]) - 1)
-    held, want = [], groups[2][-1][1] - 1
-    for g in reversed(range(len(groups[0]))):
-        if groups[0][g][1] <= want:
-            held.append(g)
-            want -= groups[0][g][1]
+
+    tail = (0, early - 1, half_chips - 1)
+    tail_chip = jnp.where(side == 0, chips - 1, 0)
+    tail_to = tail_chip * CORES + lax.rem(core + CORES - 1, CORES)
 
     def send_across(who, pieces):
         @pl.when(who)
         def _():
             for t, g, k in pieces:
                 there = jnp.where(side == 0, half_chips + k, half_chips - 1 - k)
-                send_chip(t, g, there)
+                if who is inner and (t, g, k) == tail:
+                    send_chip(t, g, there, range(CORES - 1))
+                else:
+                    send_chip(t, g, there)
 
     def scaled_pair(t, e, q, block, factor):
         value = (block * factor).astype(jnp.bfloat16)
@@ -357,7 +388,7 @@
             scaled_pair(0, e, q, first[e, :, at], factor_of(p, q))
 
     def early_factor(e):
-        return lambda p, q: early_inv[pl.ds(e, 1), p * pair : (p + 1) * pair]
+        return lambda p, q: early_inv[e, :, p * pair : (p + 1) * pair]
 
     def late_factor(e):
         return lambda p, q: inverse[q, 0, pl.ds(e, 1), :]
@@ -399,17 +430,18 @@
         start, size = groups[t][g]
         run(t, start, start + size, last, body)
 
-    @pl.when(inner)
-    def _():
-        acc = early_part[1 - side]
-        for k in range(1, n):
-            early_copy(peer(k), peer(k)).wait_recv()
-            acc = acc + early_got[peer(k)]
-        early_inv[...] = 1.0 / (acc / count)
-
-    pieces = [(0, e, k) for e in range(early) for k in range(half_chips)]
+    def early_inverse(i):
+        @pl.when(inner)
+        def _():
+            acc = early_part[1 - side, early_some[i]]
+            for k in range(1, n):
+                early_copy(i, peer(k), peer(k)).wait_recv()
+                acc = acc + early_got[peer(k), early_some[i]]
+            early_inv[early_some[i]] = 1.0 / (acc / count)
+
+    early_inverse(0)
+    pieces = [(0, e, k) for k in range(half_chips) for e in range(early)]
     outer = jnp.logical_not(inner)
-    cut = max(1, len(pieces) // 4)
     middle = experts // 2
     rest = range(early, len(groups[0]))
     low = [g for g in rest if groups[0][g][0] < middle]
@@ -421,35 +453,34 @@
             half_first(e, 1 - side, early_factor(e))
 
     early_ready(0)
-    send_across(inner, pieces[:cut])
+    if raw:
+
+        @pl.when(inner)
+        def _():
+            send_chip(0, 0, across, range(1, CORES))
+
+    send_across(inner, pieces[raw:1])
     run(0, shadow, experts, experts, sums_wide(0))
     fill(1, 0, middle)
     sums_side(0)
+    for i in range(1, len(early_some)):
+        early_inverse(i)
     for e in range(1, early):
         early_ready(e)
-    send_across(inner, pieces[cut : 2 * cut])
+    send_across(inner, pieces[1:2])
     sums_across(0)
-    send_across(inner, pieces[2 * cut : 3 * cut])
+    send_across(inner, pieces[2:4])
     run(1, 0, middle, middle, sums_wide(1))
     fill(0, early, middle)
     fill(2, 0, experts)
     sums_back(0)
-    send_across(inner, pieces[3 * cut :])
+    send_across(inner, pieces[4:])
     sums_done(0)
-
-    def send_gate_side(g):
-        if g in held:
-
-            @pl.when(inner)
-            def _():
-                send_side(0, g)
-        else:
-            send_side(0, g)
 
     def next_group(g, stop):
         ready(0, g, stop, ready_wide(0))
         send_across(inner, [(0, g, 0)])
-        send_gate_side(g)
+        send_side(0, g)
 
     for g in low:
         next_group(g, middle)
@@ -462,7 +493,7 @@
             half_first(e, 1 - side, late_factor(e))
 
     for g in range(early):
-        send_gate_side(g)
+        send_side(0, g)
     run(1, middle, experts, experts, sums_wide(1))
     fill(0, middle, experts)
     run(2, 0, experts, experts, sums_tall)
@@ -494,6 +525,17 @@
     for t in (1, 2):
         own(t, 0, experts)
 
+    if raw:
+
+        @pl.when(inner)
+        def _():
+            raw_copy().wait_recv()
+            row = inverse[me // 2, 0, pl.ds(0, 1), :]
+            mine = jnp.where(lax.rem(me, 2) == 0, row[:, :share], row[:, share:])
+            at = pl.ds(pl.multiple_of(partner * rows, rows), rows)
+            out_gate[0, at, :] = (raw_got[...] * mine).astype(jnp.bfloat16)
+            raw_copy().wait_send()
+
     for k in range(1, half):
         other = side * half + mate(k)
         router_copy(other, other).wait_recv()
@@ -501,14 +543,51 @@
     for k in range(1, owners):
         col_copy(lax.rem(home + k, owners), home).start()
 
-    before = (2, last[1] - 1)
+    @pl.when(inner)
+    def _():
+        send_chip(*tail[:2], tail_chip, range(CORES - 1, CORES))
+
+    def kept(t, g, other):
+        facing_chip = (other // CORES == across) & inner
+        if (t, g) == last:
+            return facing_chip
+        if raw and (t, g) == (0, 0):
+            return facing_chip & (other == partner)
+        return None
+
+    def unless(skip, body):
+        if skip is None:
+            body()
+        else:
+            pl.when(jnp.logical_not(skip))(body)
+
+    outers = [c for c in range(half_chips - 1)]
+
+    @pl.when(inner)
+    def _():
+        for t in range(3):
+            for g in range(len(groups[t])):
+
+                @pl.loop(0, half)
+                def _(m):
+                    other = (1 - side) * half + m
+                    skip = kept(t, g, other)
+                    if (t, g) == tail[:2]:
+                        skip = (other == tail_to) if skip is None else skip | (other == tail_to)
+                    unless(skip, lambda: block_copy(t, g, other, me).wait_send())
+
+        for i in outers:
+            there = jnp.where(side == 0, i, chips - 1 - i)
+            for c in range(CORES):
+                pl.semaphore_signal(
+                    through, inc=1, device_id={"rows": there * CORES + c}, device_id_type=MESH
+                )
+
+        block_copy(*tail[:2], tail_to, me).wait_send()
 
     @pl.when(outer)
     def _():
-        for c in range(CORES):
-            block_copy(*before, across * CORES + c, across * CORES + c).wait_recv()
-        for g in held:
-            send_side(0, g)
+        pl.semaphore_wait(through, CORES)
 
     for k in range(half_chips):
         send_across(outer, [(t, g, k) for t in range(3) for g in range(len(groups[t]))])
@@ -527,11 +606,12 @@
             total_copy(s, mate(k), member).wait_send()
     for s in range(2):
         half_copy(s).wait_send()
-    for to in reach:
-
-        @pl.when(me != to)
-        def _():
-            early_copy(to, me).wait_send()
+    for i in range(len(early_some)):
+        for to in reach:
+
+            @pl.when(me != to)
+            def _():
+                early_copy(i, to, me).wait_send()
 
     for t in range(3):
         for g in range(len(groups[t])):
@@ -539,22 +619,10 @@
             @pl.loop(1, n)
             def _(k):
                 other = peer(k)
-                facing_chip = other // CORES == across
-                if (t, g) == before:
-
-                    @pl.when(jnp.logical_not(facing_chip & outer))
-                    def _():
-                        block_copy(t, g, other, other).wait_recv()
-
-                    block_copy(t, g, other, me).wait_send()
-                elif (t, g) == last:
-
-                    @pl.when(jnp.logical_not(facing_chip & inner))
-                    def _():
-                        block_copy(t, g, other, other).wait_recv()
-                        block_copy(t, g, other, me).wait_send()
-                else:
-                    block_copy(t, g, other, other).wait_recv()
+                unless(kept(t, g, other), lambda: block_copy(t, g, other, other).wait_recv())
+
+                @pl.when(jnp.logical_not(inner & (other // half != side)))
+                def _():
                     block_copy(t, g, other, me).wait_send()
 
 
@@ -666,9 +734,10 @@
             pltpu.VMEM((slots, width, rows), f32),
             pltpu.VMEM((2, n, experts, rows, share), bf16),
             pltpu.VMEM((n, experts, share, rows), bf16),
-            pltpu.VMEM((2, early, width // 2), f32),
-            pltpu.VMEM((n, early, width // 2), f32),
-            pltpu.VMEM((early, width // 2), f32),
+            pltpu.VMEM((2, early, 1, width // 2), f32),
+            pltpu.VMEM((n, early, 1, width // 2), f32),
+            pltpu.VMEM((early, 1, width // 2), f32),
+            pltpu.VMEM((rows, share), f32),
             pltpu.VMEM((half, 3, experts, pair), f32),
             pltpu.VMEM((half, 3, experts, pair), f32),
             pltpu.VMEM((3, experts, pair), f32),
@@ -679,8 +748,9 @@
             pltpu.VMEM((1, rows), f32),
             pltpu.VMEM((columns, rows), bf16),
             dma((4, max(slots, 2, early))),
-            dma((n,)),
-            dma((n,)),
+            dma((2, n)),
+            dma((2, n)),
+            dma((2,)),
             dma((2, half)),
             dma((2, half)),
             dma((2,)),
@@ -695,6 +765,7 @@
             dma((owners,)),
             dma((total_groups, n)),
             dma((total_groups, n)),
+            pltpu.SemaphoreType.REGULAR,
         ],
         compiler_params=pltpu.CompilerParams(
             collective_id=0, has_side_effects=True, vmem_limit_bytes=38 * 1024 * 1024

time: 553 us -> 553 us (level)
  no operation moved by 1% of the time
where the time goes in v5:
time: 553 us; the launch traced here: 552 us
  Pallas kernels  551 us (100%)
    pallas_call x1, Pallas kernels, local(): pl.pallas_call(functools.partial(exchange, n, owners), name='exchange', o...  397 us
    pallas_call x1, Pallas kernels, local(): pl.pallas_call(functools.partial(late_exchange, n), name='late_exchange',...  144 us

profile of v5, /device:TPU:9, one launch (start us, length us, event | category | flops | bytes accessed | tf_op | source)
XLA Modules:
  0.0 552.3 jit_solution(1604447098186041547)
XLA Ops:
  0.6 396.8 %exchange.1 = (bf16[16,2048,128]{2,1,0:T(8,128)(2,1)S(1)}, bf16[16,2048,128]{2,1,0:T(8,128)(2,1)S(1)}, bf16[16,128,2048]{2,1,0:T(8,128)(2,1)S(1)}, f32[16,128]{1...) custom-call(f32[16,256,1024]{2,1,0:T(8,128)} %gate.1, ...), custom_call_target="tpu_custom_call" | custom-call | tf_op jit(solution)/shard_map/exchange/pallas_call | solution.py:725
  397.5 8.6 %write_back.1 = (bf16[16,2048,128]{2,1,0:T(8,128)(2,1)}, bf16[16,2048,128]{2,1,0:T(8,128)(2,1)}, bf16[16,128,2048]{2,1,0:T(8,128)(2,1)}, f32[16,128]{1,0:T(8,128...) custom-call(bf16[16,2048,128]{2,1,0:T(8,128)(2,1)S(1)} %get-tuple-element.22.refs_0_, ...), custom_call_target="tpu_custom_call" | custom-call | tf_op jit(solution)/shard_map/write_back/pallas_call | solution.py:774
  406.1 0.0 copy-start
  406.1 0.7 copy-done
  406.8 144.5 %late_exchange.1.late_got = bf16[2,8,128,256]{3,2,1,0:T(8,128)(2,1)S(1)} custom-call(bf16[2,8,128,256]{3,2,1,0:T(8,128)(2,1)S(1)} %get-tuple-element.31.late_send, f32[16,128]{1,0:T(8,128)S(1)} %copy-done), custom_call_target="tpu_custom_call" | custom-call | tf_op jit(solution)/shard_map/late_exchange/pallas_call | solution.py:783
  551.3 1.0 late_place.1
Async XLA Ops:
  406.1 0.7 copy-start

commit v6 on v5

--- a/solution.py
+++ b/solution.py
@@ -10,7 +10,7 @@
 CORES = 2
 SLOTS = 4
 EARLY = 3
-SHADOW = 6
+SHADOW = 10
 CHUNKS = 4
 GROUPS = 4
 MESH = pl.DeviceIdType.MESH

time: 553 us -> 552 us (level)
  no operation moved by 1% of the time
where the time goes in v6:
time: 552 us
  Pallas kernels  551 us (100%)
    pallas_call x1, Pallas kernels, local(): pl.pallas_call(functools.partial(exchange, n, owners), name='exchange', o...  397 us
    pallas_call x1, Pallas kernels, local(): pl.pallas_call(functools.partial(late_exchange, n), name='late_exchange',...  144 us

profile of v6, /device:TPU:9, one launch (start us, length us, event | category | flops | bytes accessed | tf_op | source)
XLA Modules:
  0.0 552.1 jit_solution(4478476839608838562)
XLA Ops:
  0.6 396.6 %exchange.1 = (bf16[16,2048,128]{2,1,0:T(8,128)(2,1)S(1)}, bf16[16,2048,128]{2,1,0:T(8,128)(2,1)S(1)}, bf16[16,128,2048]{2,1,0:T(8,128)(2,1)S(1)}, f32[16,128]{1...) custom-call(f32[16,256,1024]{2,1,0:T(8,128)} %gate.1, ...), custom_call_target="tpu_custom_call" | custom-call | tf_op jit(solution)/shard_map/exchange/pallas_call | solution.py:725
  397.2 8.6 %write_back.1 = (bf16[16,2048,128]{2,1,0:T(8,128)(2,1)}, bf16[16,2048,128]{2,1,0:T(8,128)(2,1)}, bf16[16,128,2048]{2,1,0:T(8,128)(2,1)}, f32[16,128]{1,0:T(8,128...) custom-call(bf16[16,2048,128]{2,1,0:T(8,128)(2,1)S(1)} %get-tuple-element.22.refs_0_, ...), custom_call_target="tpu_custom_call" | custom-call | tf_op jit(solution)/shard_map/write_back/pallas_call | solution.py:774
  405.9 0.0 copy-start
  405.9 0.7 copy-done
  406.6 144.5 %late_exchange.1.late_got = bf16[2,8,128,256]{3,2,1,0:T(8,128)(2,1)S(1)} custom-call(bf16[2,8,128,256]{3,2,1,0:T(8,128)(2,1)S(1)} %get-tuple-element.31.late_send, f32[16,128]{1,0:T(8,128)S(1)} %copy-done), custom_call_target="tpu_custom_call" | custom-call | tf_op jit(solution)/shard_map/late_exchange/pallas_call | solution.py:783
  551.1 1.0 late_place.1
Async XLA Ops:
  405.9 0.7 copy-start

commit v7 on v6

--- a/solution.py
+++ b/solution.py
@@ -10,7 +10,7 @@
 CORES = 2
 SLOTS = 4
 EARLY = 3
-SHADOW = 10
+SHADOW = 11
 CHUNKS = 4
 GROUPS = 4
 MESH = pl.DeviceIdType.MESH

time: 552 us -> 552 us (level)
  no operation moved by 1% of the time
where the time goes in v7:
time: 552 us
  Pallas kernels  551 us (100%)
    pallas_call x1, Pallas kernels, local(): pl.pallas_call(functools.partial(exchange, n, owners), name='exchange', o...  397 us
    pallas_call x1, Pallas kernels, local(): pl.pallas_call(functools.partial(late_exchange, n), name='late_exchange',...  144 us

profile of v7, /device:TPU:9, one launch (start us, length us, event | category | flops | bytes accessed | tf_op | source)
XLA Modules:
  0.0 552.1 jit_solution(17495667520267899661)
XLA Ops:
  0.6 396.6 %exchange.1 = (bf16[16,2048,128]{2,1,0:T(8,128)(2,1)S(1)}, bf16[16,2048,128]{2,1,0:T(8,128)(2,1)S(1)}, bf16[16,128,2048]{2,1,0:T(8,128)(2,1)S(1)}, f32[16,128]{1...) custom-call(f32[16,256,1024]{2,1,0:T(8,128)} %gate.1, ...), custom_call_target="tpu_custom_call" | custom-call | tf_op jit(solution)/shard_map/exchange/pallas_call | solution.py:725
  397.2 8.6 %write_back.1 = (bf16[16,2048,128]{2,1,0:T(8,128)(2,1)}, bf16[16,2048,128]{2,1,0:T(8,128)(2,1)}, bf16[16,128,2048]{2,1,0:T(8,128)(2,1)}, f32[16,128]{1,0:T(8,128...) custom-call(bf16[16,2048,128]{2,1,0:T(8,128)(2,1)S(1)} %get-tuple-element.22.refs_0_, ...), custom_call_target="tpu_custom_call" | custom-call | tf_op jit(solution)/shard_map/write_back/pallas_call | solution.py:774
  405.9 0.0 copy-start
  405.9 0.7 copy-done
  406.6 144.5 %late_exchange.1.late_got = bf16[2,8,128,256]{3,2,1,0:T(8,128)(2,1)S(1)} custom-call(bf16[2,8,128,256]{3,2,1,0:T(8,128)(2,1)S(1)} %get-tuple-element.31.late_send, f32[16,128]{1,0:T(8,128)S(1)} %copy-done), custom_call_target="tpu_custom_call" | custom-call | tf_op jit(solution)/shard_map/late_exchange/pallas_call | solution.py:783
  551.1 1.0 late_place.1
Async XLA Ops:
  405.9 0.7 copy-start
